TPU v7x, 16 devices: a whole 2x2x2 slice. The times are simulated.
16 devices in a mesh: sp: 16 (over z, y, x, core).
Axes of the slice: x: 2, y: 2, z: 2, core: 2. Of those that a mesh axis runs over, the one named last changes fastest.
Arguments:
- x: bfloat16 [4, 2048, 1024], P(None, 'sp')
- d_y: bfloat16 [4, 2048, 1024], P(None, 'sp')
- ln_gamma: bfloat16 [1024], replicated
- ln_beta: bfloat16 [1024], replicated
- w_qkv: bfloat16 [1024, 3072], replicated
- b_qkv: bfloat16 [3072], replicated
- w_out: bfloat16 [1024, 1024], replicated
- b_out: bfloat16 [1024], replicated
- head_kind: int32 [16], replicated
Outputs:
- output 1: bfloat16 [4, 2048, 1024], P(None, 'sp')
- output 2: bfloat16 [4, 2048, 1024], P(None, 'sp')
- output 3: float32 [1024], replicated
- output 4: float32 [1024], replicated
- output 5: float32 [1024, 3072], replicated
- output 6: float32 [3072], replicated
- output 7: float32 [1024, 1024], replicated
- output 8: float32 [1024], replicated
All inputs are finite; a program needn't handle non-finite values.
Results may differ from a plain program's by a relative error of at most 0.0134294.
Values are sent between devices in bfloat16 or wider.
A program may use at most 1 GiB of HBM per device.

v0:
```python
import functools
import math

import jax
import jax.numpy as jnp
from jax import lax
from jax.experimental import pallas as pl
from jax.experimental.pallas import tpu as pltpu
from jax.sharding import PartitionSpec as P

LN_EPS = 1e-5
NEG_BIG = -1e30
BF = jnp.bfloat16
F32 = jnp.float32
QB = 256
L = 128
W3 = 384
T = 512
D = 1024
DR = 1040
HR = 520
N = 16
R3, R4, R8 = range(3), range(4), range(8)
MESH = pl.DeviceIdType.MESH
H_ROWS = (0, 96, 176, 256)
W_ROWS = (0, 176, 352, 520)
O_ROWS = (0, 24, 48, 64)
S = 2048
D3 = 3072
VMEM_CAP = 63 * D * D


def dot_nn(a, b):
    return lax.dot_general(a, b, (((1,), (0,)), ((), ())), preferred_element_type=F32)


def dot_nt(a, b):
    return lax.dot_general(a, b, (((1,), (1,)), ((), ())), preferred_element_type=F32)


def dot_tn(a, b):
    return lax.dot_general(a, b, (((0,), (0,)), ((), ())), preferred_element_type=F32)


def swap_halves(a):
    return jnp.concatenate([a[:, 64:], a[:, :64]], axis=1)


def pair_halves(a, a_half, b, b_half):
    lane = lax.broadcasted_iota(jnp.int32, a.shape, 1)
    a = jnp.where(a_half == 1, swap_halves(a), a)
    b = jnp.where(b_half == 0, swap_halves(b), b)
    return jnp.where(lane < 64, a, b)


class Place:
    def __init__(self):
        self.me = lax.axis_index("sp")
        self.core, self.chip = self.me % 2, self.me // 2
        self.sib = self.me + 1 - 2 * self.core
        bits = (self.chip % 2, self.chip // 2 % 2, self.chip // 4)
        self.step = [(1 - 2 * v) * w for v, w in zip(bits, (1, 2, 4))]

    def chip_at(self, axes):
        out = self.chip
        for a in axes:
            out = out + self.step[a]
        return out

    def next_dev(self, axis):
        return self.me + 2 * self.step[axis]


def rcopy(src, dst, send, recv, dev):
    return pltpu.make_async_remote_copy(
        src_ref=src, dst_ref=dst, send_sem=send, recv_sem=recv, device_id=(dev,), device_id_type=MESH)


def subsets(axes):
    out = [()]
    for a in axes:
        out += [v + (a,) for v in out]
    return out


class Tree:
    def __init__(self, place, own, slot, seven, send, recv):
        self.place, self.own, self.slot, self.seven, self.send, self.recv = place, own, slot, seven, send, recv
        self.entries = []
        for s in R3:
            for p in R3:
                order = [(p + j) % 3 for j in R3]
                for sub in subsets(order[:s]):
                    self.entries.append((p, order[s], sub))

    def copy(self, e):
        p, axis, sub = e
        i = self.entries.index(e)
        at = self.slot(self.place.chip_at(sub), p)
        return rcopy(at if sub else self.own(p), at, self.send, self.recv.at[i], self.place.next_dev(axis))

    def start_own(self, levels=R3):
        for e in self.hops(0):
            if (e[1] - e[0]) % 3 in levels:
                self.copy(e).start()

    def arrive(self, e):
        p, axis, sub = e
        got = sub + (axis,)
        chip = self.place.chip_at(got)
        at = self.slot(chip, p)
        i = self.entries.index(e)
        rcopy(at, at, self.send, self.recv.at[i], self.place.next_dev(axis)).wait_recv()
        for n in self.entries:
            if n[0] == p and n[2] == got:
                self.copy(n).start()
        return chip, p

    def hops(self, n):
        return [e for e in self.entries if len(e[2]) == n]

    def finish(self):
        rcopy(self.seven, self.seven, self.send, self.recv.at[0], self.place.me).wait_send()


def barrier_signal(place):
    sem = pltpu.get_barrier_semaphore()
    for r in range(1, N):
        pl.semaphore_signal(sem, inc=1, device_id=((place.me + r) % N,), device_id_type=MESH)


def barrier_wait():
    pl.semaphore_wait(pltpu.get_barrier_semaphore(), N - 1)


def head_places(kind_ref):
    pos, zeros, ones = [], 0, 8
    for n in range(N):
        k = kind_ref[n]
        pos.append(jnp.where(k == 0, zeros, ones))
        zeros, ones = zeros + 1 - k, ones + k
    return pos


class Exchange:
    def __init__(self, place, src, dst, rest, send, recv):
        self.place, self.src, self.dst, self.send, self.recv = place, src, dst, send, recv
        self.rest = rest

    def start(self, first=1, end=N):
        me = self.place.me
        for r in range(first, end):
            to = (me + r) % N
            rcopy(self.src(to), self.dst(me), self.send, self.recv, to).start()

    def wait(self):
        rcopy(self.rest, self.rest, self.send, self.recv, self.place.me).wait_recv()

    def finish(self):
        rcopy(self.rest, self.rest, self.send, self.recv, self.place.me).wait_send()


def gather_heads(recv_at, pos, b, m):
    pa, pb = pos[2 * m], pos[2 * m + 1]
    k, j = b // 2, b % 2
    a = recv_at(j, 2 * (pa % 8) + k)
    c = recv_at(j, 2 * (pb % 8) + k)
    return pair_halves(a, pa // 8, c, pb // 8)


def span(tab):
    return lambda p: pl.ds(tab[p], tab[p + 1] - tab[p])


def centre(xb):
    xf = xb.astype(F32)
    cen = xf - jnp.mean(xf, axis=-1, keepdims=True)
    rstd = lax.rsqrt(jnp.mean(cen * cen, axis=-1, keepdims=True) + LN_EPS)
    return xf, cen * rstd, rstd


def layer_kernel(kind_ref, x_ref, dy_ref, gamma_ref, beta_ref, bout_ref, bqkv_ref, wqkv_hbm, wout_hbm,
                 y_ref, dx_ref, small_ref, dwg_ref, dwo_ref,
                 hg_ref, out_ref, wout_ref, wp_ref, do_ref, dog_ref, w_ref, bias_ref, qkv_ref, dqkv_ref, qt_ref, dot_ref,
                 dkt_ref, dvt_ref, s_f, p_f, ds_f, s_g, p_g, ds_g, so_ref, sd_ref, ro_ref, rd_ref, o_nat, dqkv_nat,
                 dwp_ref, dws_ref, part_ref, px_ref, acc_ref, rs0_ref, rs1_ref, rs2_ref, sm_ref, sm_out,
                 loc, sib_send, sib_recv, h_send, h_recv, do_send, do_recv, o_send, o_recv, d_send, d_recv,
                 s_send, s_recv, w_send, w_recv, g_send, g_recv, ws_send, ws_recv, gs_send, gs_recv, r_send, r_recv):
    pc = Place()
    barrier_signal(pc)

    def w_load(r):
        return pltpu.make_async_copy(wqkv_hbm.at[r * T:(r + 1) * T], dqkv_nat, loc.at[r])

    wo_load = pltpu.make_async_copy(wout_hbm, wout_ref, loc.at[2])
    w_load(0).start()
    wo_load.start()
    gamma = gamma_ref[...].reshape(1, D).astype(F32)
    beta = beta_ref[...].reshape(1, D).astype(F32)
    bout = bout_ref[...].reshape(1, D).astype(F32)
    bqkv = bqkv_ref[...].reshape(1, D3).astype(F32)

    def rows_of(core):
        return pl.ds(pl.multiple_of(core * L, L), L)

    def norm(xb):
        return (centre(xb)[1] * gamma + beta).astype(BF)

    def sib_copy(j):
        return rcopy(out_ref.at[j], hg_ref.at[pc.chip, j, rows_of(pc.core)], sib_send.at[j], sib_recv.at[j], pc.sib)

    for j in range(2):
        out_ref[j] = norm(x_ref[2 * (1 - pc.core) + j])
    for j in range(2):
        hg_ref[pc.chip, j, rows_of(pc.core)] = norm(x_ref[2 * pc.core + j])
    barrier_wait()
    for j in range(2):
        sib_copy(j).start()

    h_rows, w_rows, o_rows = span(H_ROWS), span(W_ROWS), span(O_ROWS)

    def h_tree(j):
        slot = lambda c, p: hg_ref.at[c, j, h_rows(p)]
        return Tree(pc, lambda p: slot(pc.chip, p), slot, hg_ref.at[0:7, j], h_send.at[j], h_recv.at[j])

    def sib_arrive(j):
        at = hg_ref.at[pc.chip, j, rows_of(1 - pc.core)]
        rcopy(at, at, sib_send.at[j], sib_recv.at[j], pc.sib).wait_recv()

    do_out = do_ref.reshape(N, 2, L, L)

    def swap(src, dst, send, recv, j):
        return Exchange(pc, lambda t: src(t, j), lambda t: dst.at[j, t], dst.at[j, 0:N - 1], send.at[j], recv.at[j])

    def do_swap(j):
        return swap(lambda t, j: do_out.at[t, j], dog_ref, do_send, do_recv, j)

    def o_swap(j):
        return swap(lambda t, j: so_ref.at[j, t], ro_ref, o_send, o_recv, j)

    def d_swap(j):
        return swap(lambda t, j: sd_ref.at[j, t], rd_ref, d_send, d_recv, j)

    trees = [h_tree(0), h_tree(1)]
    sib_arrive(0)
    trees[0].start_own()
    pos = head_places(kind_ref)
    perm = []
    for j in range(N):
        v = 0
        for n in range(1, N):
            v = v + jnp.where(pos[n] == j, n, 0)
        perm.append(v)
    f = g = 0
    for c in R8:
        f = f + jnp.where(pc.chip == c, perm[c], 0)
        g = g + jnp.where(pc.chip == c, perm[8 + c], 0)
    wo_load.wait()
    dy_all = dy_ref[...].reshape(T, D)
    for c in R4:
        for u in range(2):
            wp_ref[u * L:u * L + 64] = wout_ref[perm[2 * c + u]]
            wp_ref[u * L + 64:u * L + L] = wout_ref[perm[8 + 2 * c + u]]
        d = dot_nt(dy_all, wp_ref[...]).astype(BF)
        for u in range(2):
            do_ref[2 * c + u] = d[:, u * L:(u + 1) * L].reshape(4, L, L)
    for e in trees[0].hops(0):
        trees[0].arrive(e)
    do_swap(0).start()
    for j in range(2):
        dog_ref[j, pc.me] = do_out[pc.me, j]

    def w_cols(t, k, head):
        out = None
        for m in R8:
            cur = dqkv_nat[k * L:(k + 1) * L, t * D + m * L:t * D + (m + 1) * L]
            out = cur if out is None else jnp.where(head // 2 == m, cur, out)
        return out

    for r in range(2):
        w_load(r).wait()
        for t in R3:
            for k in R4:
                w_ref[r * T + k * L:r * T + (k + 1) * L, t * L:(t + 1) * L] = pair_halves(
                    w_cols(t, k, f), f % 2, w_cols(t, k, g), g % 2)
        if r == 0:
            w_load(1).start()
    for t in R3:
        halves = []
        for head in (f, g):
            out = None
            for m in R8:
                cur = bqkv[:, t * D + m * L:t * D + (m + 1) * L]
                out = cur if out is None else jnp.where(head // 2 == m, cur, out)
            halves += [out, head % 2]
        bias_ref[:, t * L:(t + 1) * L] = jnp.broadcast_to(pair_halves(*halves), (8, L))
    dwp_ref[...] = jnp.zeros_like(dwp_ref)
    for e in trees[0].hops(1):
        trees[0].arrive(e)
    sib_arrive(1)
    trees[1].start_own()

    lane = lax.broadcasted_iota(jnp.int32, (QB, L), 1)
    row_i = lax.broadcasted_iota(jnp.int32, (QB, QB), 0)
    col_i = lax.broadcasted_iota(jnp.int32, (QB, QB), 1)

    def head_block(j, i, hd):
        s_ref, p_ref, ds_ref = ((s_f, p_f, ds_f), (s_g, p_g, ds_g))[hd]
        first = 0 if hd == 0 else max(0, i - 2)
        blocks = range(first, i + 1)
        mine = (lane < 64) if hd == 0 else (lane >= 64)
        qi = qkv_ref[i * QB:(i + 1) * QB, 0:L] * BF(0.125)
        doi = dog_ref[j, 2 * i:2 * i + 2].reshape(QB, L)
        qm = jnp.where(mine, qi, BF(0))
        dom = jnp.where(mine, doi, BF(0))
        k_at = lambda kb: qkv_ref[kb * QB:(kb + 1) * QB, L:2 * L]
        v_at = lambda kb: qkv_ref[kb * QB:(kb + 1) * QB, 2 * L:3 * L]
        at = lambda kb: slice((kb - first) * QB, (kb - first + 1) * QB)
        mx = None
        for kb in blocks:
            s = dot_nt(qm, k_at(kb))
            if kb == i:
                s = jnp.where(col_i <= row_i, s, NEG_BIG)
            if hd == 1 and kb == i - 2:
                s = jnp.where(col_i > row_i, s, NEG_BIG)
            s_ref[:, at(kb)] = s
            cur = jnp.maximum(s[:, :L], s[:, L:])
            mx = cur if mx is None else jnp.maximum(mx, cur)
        m = jnp.max(mx, axis=1, keepdims=True)
        ls = None
        for kb in blocks:
            e = jnp.exp(s_ref[:, at(kb)] - m)
            s_ref[:, at(kb)] = e
            cur = e[:, :L] + e[:, L:]
            ls = cur if ls is None else ls + cur
        rl = 1.0 / jnp.sum(ls, axis=1, keepdims=True)
        acc = None
        for kb in blocks:
            p_ = s_ref[:, at(kb)] * rl
            s_ref[:, at(kb)] = p_
            pb = p_.astype(BF)
            p_ref[:, at(kb)] = pb
            cur = dot_nn(pb, v_at(kb))
            acc = cur if acc is None else acc + cur
        dsum = jnp.sum(dom.astype(F32) * acc, axis=1, keepdims=True)
        dq = None
        for kb in blocks:
            dp = dot_nt(dom, v_at(kb)).astype(BF).astype(F32)
            ds = (s_ref[:, at(kb)] * (dp - dsum)).astype(BF)
            ds_ref[:, at(kb)] = ds
            cur = dot_nn(ds, k_at(kb))
            dq = cur if dq is None else dq + cur
        hr = slice(hd * 64, hd * 64 + 64)
        n = len(blocks) * QB
        keys = slice(first * QB, first * QB + n)
        dvt_ref[hr, keys] += dot_nn(dot_ref[hr, i * QB:(i + 1) * QB], p_ref[:, :n])
        dkt_ref[hr, keys] += dot_nn(qt_ref[hr, i * QB:(i + 1) * QB], ds_ref[:, :n])
        return acc, dq * 0.125

    def batch_step(j, carry):
        last = h_tree(j)
        for e in last.hops(2):
            last.arrive(e)
        do_swap(j).wait()

        @pl.when(j == 1)
        def _():
            o_swap(0).start()
            d_swap(0).start()

        def qkv_step(r, c):
            rows = hg_ref[pl.ds(2 * r, 2), j].reshape(T, D)
            out = dot_nn(rows, w_ref[...]) + bias_ref[0:1, :]
            qkv_ref[pl.ds(pl.multiple_of(r * T, T), T), :] = out.astype(BF)
            return c

        lax.fori_loop(0, 4, qkv_step, 0)

        for i in R8:
            qs = qkv_ref[i * QB:(i + 1) * QB, 0:L] * BF(0.125)
            qt_ref[:, i * QB:(i + 1) * QB] = qs.T
            dot_ref[:, i * QB:(i + 1) * QB] = dog_ref[j, 2 * i:2 * i + 2].reshape(QB, L).T
        dkt_ref[...] = jnp.zeros_like(dkt_ref)
        dvt_ref[...] = jnp.zeros_like(dvt_ref)
        for i in R8:
            of, dqf = head_block(j, i, 0)
            og, dqg = head_block(j, i, 1)
            o = jnp.where(lane < 64, of, og).astype(BF)
            dq = jnp.where(lane < 64, dqf, dqg).astype(BF)
            for u in range(2):
                so_ref[j, 2 * i + u] = o[u * L:(u + 1) * L]
                sd_ref[j, 2 * i + u, 0] = dq[u * L:(u + 1) * L]
            dqkv_ref[i * QB:(i + 1) * QB, 0:L] = dq
            if i == 3:
                @pl.when(j == 0)
                def _():
                    for e in trees[1].hops(0):
                        trees[1].arrive(e)
                    do_swap(1).start()

        for t, src in ((1, dkt_ref), (2, dvt_ref)):
            for n in range(N):
                d = src[:, n * L:(n + 1) * L].T.astype(BF)
                sd_ref[j, n, t] = d
                dqkv_ref[n * L:(n + 1) * L, t * L:(t + 1) * L] = d
        ro_ref[j, pc.me] = so_ref[j, pc.me]
        rd_ref[j, pc.me] = sd_ref[j, pc.me]

        @pl.when(j == 0)
        def _():
            for e in trees[1].hops(1):
                trees[1].arrive(e)

        @pl.when(j == 1)
        def _():
            o_swap(1).start()

        def dw_step(r, c):
            cols = pl.ds(pl.multiple_of(r * QB, QB), QB)
            dwp_ref[cols, :] += dot_tn(hg_ref[:, j, :, cols].reshape(S, QB), dqkv_ref[...])
            return c

        lax.fori_loop(0, 4, dw_step, 0)
        dwp_ref[D:D + 1, :] += jnp.sum(dqkv_ref[...].astype(F32), axis=0, keepdims=True)
        return carry

    lax.fori_loop(0, 2, batch_step, 0)

    def half_of(core):
        return dwp_ref.at[pl.ds(pl.multiple_of(core * HR, 8), HR)]

    def to_sib(n, src, dst, send, recv):
        cp = rcopy(src, dst, send.at[n], recv.at[n], pc.sib)
        cp.start()
        return cp

    half = to_sib(2, half_of(1 - pc.core), dws_ref, sib_send, sib_recv)
    for j in range(2):
        trees[j].finish()
        do_swap(j).finish()
    w_flat = hg_ref.reshape(2 * S, D)
    w_loads = [pltpu.make_async_copy(wqkv_hbm.at[:, t * D:(t + 1) * D], w_flat.at[t * D:(t + 1) * D], loc.at[3 + t]) for t in R3]
    for cp in w_loads:
        cp.start()
    half.wait_recv()
    dws_ref[...] += half_of(pc.core)[...]

    def w_slot(c, p, core=pc.core):
        return dwg_ref.at[c, core, w_rows(p)]

    def g_slot(c, p, core=pc.core):
        return dwo_ref.at[core, c, o_rows(p)]

    wtree = Tree(pc, lambda p: dws_ref.at[w_rows(p)], w_slot, dwg_ref.at[0:7, pc.core], w_send.at[0], w_recv)
    wtree.start_own((0,))
    keep_w = pltpu.make_async_copy(dws_ref, dwg_ref.at[pc.chip, pc.core], loc.at[0])
    keep_w.start()
    for p in R3:
        to_sib(0, dws_ref.at[w_rows(p)], w_slot(pc.chip, p), ws_send, ws_recv)

    for j in range(2):
        o_swap(j).wait()
    for b in R4:
        for m in R8:
            o_nat[b * L:(b + 1) * L, m * L:(m + 1) * L] = gather_heads(lambda j, q: ro_ref[j, q], pos, b, m)

    def wout_part(core, c):
        cols = pl.ds(pl.multiple_of(core * T + c * QB, QB), QB)
        return dot_tn(o_nat[:, cols], dy_all)

    for c in range(2):
        part_ref[c * QB:(c + 1) * QB] = wout_part(1 - pc.core, c)
    xp = to_sib(3, part_ref, px_ref, sib_send, sib_recv)
    for c in range(2):
        acc_ref[4 * c:4 * c + 4] = wout_part(pc.core, c).reshape(4, 64, D)
    xp.wait_recv()
    acc_ref[...] += px_ref[...].reshape(8, 64, D)

    bufs = (rs0_ref, rs1_ref, rs2_ref)

    def reduce_step(s, wait):
        for p in R3:
            order = [(p + j) % 3 for j in R3]
            if wait:
                at = bufs[s].at[:, o_rows(p)]
                rcopy(at, at, r_send.at[0], r_recv.at[s * 3 + p], pc.sib).wait_recv()
            for i, sub in enumerate(subsets(order[s + 1:])):
                if wait:
                    acc_ref[pc.chip_at(sub), o_rows(p)] += bufs[s][i, o_rows(p)]
                else:
                    rcopy(acc_ref.at[pc.chip_at((order[s],) + sub), o_rows(p)], bufs[s].at[i, o_rows(p)],
                          r_send.at[0], r_recv.at[s * 3 + p], pc.next_dev(order[s])).start()

    reduce_step(0, False)
    wtree.start_own((1, 2))
    def pass_on(tree, slot, n, send, recv):
        for e in tree.hops(n):
            c, p = tree.arrive(e)
            to_sib(0, slot(c, p), slot(c, p), send, recv)

    dbo = jnp.zeros((1, D), F32)
    for b in R4:
        rows = slice(b * L, (b + 1) * L)
        y_ref[b] = (x_ref[b].astype(F32) + dot_nn(o_nat[rows], wout_ref.reshape(D, D)[...]) + bout).astype(BF)
        dbo += jnp.sum(dy_ref[b].astype(F32), axis=0, keepdims=True)
    reduce_step(0, True)
    reduce_step(1, False)
    d_swap(1).start(1, 9)
    reduce_step(1, True)
    reduce_step(2, False)
    d_swap(1).start(9)
    reduce_step(2, True)
    gtree = Tree(pc, lambda p: acc_ref.at[pc.chip, o_rows(p)], g_slot, dwo_ref.at[pc.core, 0:7], g_send.at[0], g_recv)
    gtree.start_own()
    keep_g = pltpu.make_async_copy(acc_ref.at[pc.chip], dwo_ref.at[pc.core, pc.chip], loc.at[1])
    keep_g.start()
    for p in R3:
        to_sib(0, acc_ref.at[pc.chip, o_rows(p)], g_slot(pc.chip, p), gs_send, gs_recv)

    pass_on(wtree, w_slot, 0, ws_send, ws_recv)
    for j in range(2):
        d_swap(j).wait()

    def spread(b, c):
        rows = pl.ds(pl.multiple_of(b * L, L), L)
        for m in R8:
            for t in R3:
                dqkv_nat[rows, t * D + m * L:t * D + (m + 1) * L] = gather_heads(lambda j, q: rd_ref[j, q, t], pos, b, m)
        return c

    def back(b, c):
        dg, db = c
        rows = pl.ds(pl.multiple_of(b * L, L), L)
        _, xhat, rstd = centre(x_ref[b])
        dh = None
        for t in R3:
            cur = dot_nt(dqkv_nat[rows, t * D:(t + 1) * D], w_flat[t * D:(t + 1) * D])
            dh = cur if dh is None else dh + cur
        dh = dh.astype(BF).astype(F32)
        dxh = dh * gamma
        m1 = jnp.mean(dxh, axis=-1, keepdims=True)
        m2 = jnp.mean(dxh * xhat, axis=-1, keepdims=True)
        dx_ref[b] = (dy_ref[b].astype(F32) + rstd * (dxh - m1 - xhat * m2)).astype(BF)
        return dg + jnp.sum(dh * xhat, axis=0, keepdims=True), db + jnp.sum(dh, axis=0, keepdims=True)

    lax.fori_loop(0, 4, spread, 0)
    for cp in w_loads:
        cp.wait()
    dgb = lax.fori_loop(0, 2, back, (jnp.zeros((1, D), F32), jnp.zeros((1, D), F32)))
    pass_on(gtree, g_slot, 0, gs_send, gs_recv)
    dg, db = lax.fori_loop(2, 4, back, dgb)
    row = lax.broadcasted_iota(jnp.int32, (4, D), 0)
    sm_out[...] = jnp.where(row == 0, dg, jnp.where(row == 1, db, jnp.where(row == 2, dbo, 0.0)))
    sm_ref[pc.me] = sm_out[...]
    s_swap = Exchange(pc, lambda t: sm_out, lambda t: sm_ref.at[t], sm_ref.at[0:N - 1], s_send.at[0], s_recv.at[0])
    s_swap.start()
    pass_on(wtree, w_slot, 1, ws_send, ws_recv)
    pass_on(gtree, g_slot, 1, gs_send, gs_recv)
    s_swap.wait()
    tot = sm_ref[0]
    for n in range(1, N):
        tot = tot + sm_ref[n]
    small_ref[...] = tot
    pass_on(gtree, g_slot, 2, gs_send, gs_recv)
    pass_on(wtree, w_slot, 2, ws_send, ws_recv)
    for tree, at, got, send, recv in (
            (wtree, dwg_ref.at[:, pc.core], dwg_ref.at[:, 1 - pc.core], ws_send, ws_recv),
            (gtree, dwo_ref.at[pc.core], dwo_ref.at[1 - pc.core], gs_send, gs_recv)):
        rcopy(got, got, send.at[0], recv.at[0], pc.sib).wait_recv()
        rcopy(at, at, send.at[0], recv.at[0], pc.sib).wait_send()
        tree.finish()
    for j in range(2):
        sib_copy(j).wait_send()
        o_swap(j).finish()
        d_swap(j).finish()
    s_swap.finish()
    half.wait_send()
    xp.wait_send()
    rcopy(acc_ref.at[0:7], acc_ref.at[0:7], r_send.at[0], r_recv.at[0], pc.sib).wait_send()
    keep_w.wait()
    keep_g.wait()


def layer_call(kind, x, dy, gamma, beta, bout, bqkv, wqkv, wout):
    vm, sm, hb = (pl.BlockSpec(memory_space=m) for m in (pltpu.VMEM, pltpu.SMEM, pl.ANY))
    sem = pltpu.SemaphoreType.DMA
    tok = jax.ShapeDtypeStruct((4, L, D), BF)

    def pair(*n):
        return [sem(n), sem(n)]

    def bf(*n):
        return pltpu.VMEM(n, BF)

    def ff(*n):
        return pltpu.VMEM(n, F32)

    band = 3 * QB
    return pl.pallas_call(
        layer_kernel,
        out_shape=(tok, tok, jax.ShapeDtypeStruct((4, D), F32), jax.ShapeDtypeStruct((8, 2, HR, W3), F32),
                   jax.ShapeDtypeStruct((2, 8, 64, D), F32)),
        in_specs=[sm] + [vm] * 6 + [hb, hb],
        out_specs=(vm, vm, vm, hb, hb),
        scratch_shapes=[
            bf(8, 2, QB, D), bf(2, L, D), bf(N, 64, D), bf(QB, D), bf(8, 4, L, L), bf(2, N, L, L), bf(D, W3), ff(8, W3),
            bf(S, W3), bf(S, W3), bf(L, S), bf(L, S), ff(L, S), ff(L, S),
            ff(QB, S), bf(QB, S), bf(QB, S), ff(QB, band), bf(QB, band), bf(QB, band),
            bf(2, N, L, L), bf(2, N, 3, L, L), bf(2, N, L, L), bf(2, N, 3, L, L), bf(T, D), bf(T, D3),
            ff(DR, W3), ff(HR, W3), ff(T, D), ff(T, D), ff(8, 64, D),
            ff(4, 64, D), ff(2, 64, D), ff(1, 64, D), ff(N, 4, D), ff(4, D), sem((6,))]
        + pair(4) + [sem((2,)), sem((2, 21))] + pair(2) + pair(2) + pair(2) + pair(1)
        + [sem((1,)), sem((21,))] + [sem((1,)), sem((21,))] + pair(1) + pair(1) + [sem((1,)), sem((9,))],
        compiler_params=pltpu.CompilerParams(vmem_limit_bytes=VMEM_CAP, collective_id=0, has_side_effects=True),
        name="layer",
    )(kind, x, dy, gamma, beta, bout, bqkv, wqkv, wout)


def unpack_kernel(kind_ref, dw_hbm, dwo_hbm, y_in, dx_in, small_ref,
                  out_hbm, wo_hbm, y_out, dx_out, bias_ref, dg_ref, db_ref, dbo_ref,
                  in_ref, ob_ref, bias_in, wo_ref, y_ref, dx_ref, in_sem, out_sem, pass_in, pass_out):
    pos = head_places(kind_ref)

    def rows(r):
        return pl.ds(pl.multiple_of(r * 64, 64), 64)

    def load(r):
        return pltpu.make_async_copy(dw_hbm.at[:, rows(r)], in_ref.at[r], in_sem.at[r])

    def store(r):
        return pltpu.make_async_copy(ob_ref.at[r], out_hbm.at[rows(r)], out_sem.at[r])

    chain = ((dwo_hbm, wo_ref, wo_hbm), (y_in, y_ref, y_out), (dx_in, dx_ref, dx_out))

    def get(i):
        return pltpu.make_async_copy(chain[i][0], chain[i][1], pass_in.at[i])

    def put(i):
        return pltpu.make_async_copy(chain[i][1], chain[i][2], pass_out.at[i])

    bias_load = pltpu.make_async_copy(dw_hbm.at[:, D:D + 8], bias_in, pass_in.at[3])
    for r in R8:
        load(r).start()
    bias_load.start()

    def pick(read, t, m):
        pa, pb = pos[2 * m], pos[2 * m + 1]
        cols = slice(t * L, (t + 1) * L)
        a, b = read(pa % 8, cols), read(pb % 8, cols)
        lane = lax.broadcasted_iota(jnp.int32, a.shape, 1)
        a = jnp.where(pa // 8 == 1, pltpu.roll(a, 64, 1), a)
        b = jnp.where(pb // 8 == 0, pltpu.roll(b, 64, 1), b)
        return jnp.where(lane < 64, a, b)

    def step(r, c):
        load(r).wait()

        @pl.when(r < 8)
        def _():
            load(r + 8).start()

        @pl.when(r == 2)
        def _():
            for i in R3:
                get(i).start()

        @pl.when(r == 8)
        def _():
            for i in R3:
                get(i).wait()
                put(i).start()

        for t in R3:
            for m in R8:
                ob_ref[r, :, t * D + m * L:t * D + (m + 1) * L] = pick(lambda q, cols: in_ref[r, q, :, cols], t, m)
        store(r).start()
        return c

    lax.fori_loop(0, N, step, 0)
    bias_load.wait()
    for t in R3:
        for m in R8:
            bias_ref[t * D + m * L:t * D + (m + 1) * L] = pick(lambda q, cols: bias_in[q, :, cols], t, m)[0]
    for i, ref in enumerate((dg_ref, db_ref, dbo_ref)):
        ref[...] = small_ref[i]
    for r in range(N):
        store(r).wait()
    for i in R3:
        put(i).wait()


def unpack_call(kind, dwg, dwo, small, y, dx):
    vm, sm, hb = (pl.BlockSpec(memory_space=m) for m in (pltpu.VMEM, pltpu.SMEM, pl.ANY))
    sem = pltpu.SemaphoreType.DMA
    vec = jax.ShapeDtypeStruct((D,), F32)
    tok = jax.ShapeDtypeStruct((4, L, D), BF)
    return pl.pallas_call(
        unpack_kernel,
        in_specs=[sm, hb, hb, hb, hb, vm],
        out_specs=[hb, hb, hb, hb, vm, vm, vm, vm],
        out_shape=[jax.ShapeDtypeStruct((D, D3), F32), jax.ShapeDtypeStruct((D, D), F32), tok, tok,
                   jax.ShapeDtypeStruct((D3,), F32), vec, vec, vec],
        scratch_shapes=[
            pltpu.VMEM((N, 8, 64, W3), F32), pltpu.VMEM((N, 64, D3), F32), pltpu.VMEM((8, 8, W3), F32),
            pltpu.VMEM((D, D), F32), pltpu.VMEM((4, L, D), BF), pltpu.VMEM((4, L, D), BF),
            sem((N,)), sem((N,)), sem((4,)), sem((3,))],
        compiler_params=pltpu.CompilerParams(vmem_limit_bytes=VMEM_CAP),
        name="unpack",
    )(kind, dwg, dwo, y, dx, small)


def solution(mesh):
    tok_spec = P(None, "sp", None)

    def local_block(x, d_y, ln_gamma, ln_beta, w_qkv, b_qkv, w_out, b_out, head_kind):
        y, dx, small, dwg, dwo = layer_call(head_kind, x, d_y, ln_gamma, ln_beta, b_out, b_qkv, w_qkv, w_out.reshape(N, 64, D))
        dw, dwout, y, dx, dbias, dg, db, dbo = unpack_call(
            head_kind, dwg.reshape(8, DR, W3), dwo.reshape(D, D), small, y, dx)
        return y, dx, dg, db, dw, dbias, dwout, dbo

    return jax.shard_map(
        local_block, mesh=mesh,
        in_specs=(tok_spec, tok_spec, P(), P(), P(), P(), P(), P(), P()),
        out_specs=(tok_spec, tok_spec, P(), P(), P(), P(), P(), P()), check_vma=False)
```

profile of v0, /device:TPU:0, one launch (start us, length us, event | category | flops | bytes accessed | tf_op | source)
XLA Modules:
  0.0 217.9 jit_solution(8770964540798867807)
XLA Ops:
  0.6 203.0 %layer.1 = (bf16[4,128,1024]{2,1,0:T(8,128)(2,1)}, bf16[4,128,1024]{2,1,0:T(8,128)(2,1)}, f32[4,1024]{1,0:T(4,128)}, f32[8,2,520,384]{3,2,1,0:T(8,128)}, f32[2,8,64,1024]{3,2,1,0:T(8,128)}) custom-call(s32[16]{0:T(128)} %kind_ref.3, bf16[4,128,1024]{2,1,0:T(8,128)(2,1)} %x_ref.1, bf16[4,128,1024]{2,1,0:T(8,128)(2,1)} %dy_ref.1, bf16[1024]{0:T(1024)(128)(2,1)} %gamma_ref.1, ...), custom_call_target="tpu_custom_call" | custom-call | tf_op jit(solution)/shard_map/layer/pallas_call | solution.py:599
  203.6 14.1 %unpack.1 = (f32[1024,3072]{1,0:T(8,128)}, f32[1024,1024]{1,0:T(8,128)}, bf16[4,128,1024]{2,1,0:T(8,128)(2,1)}, bf16[4,128,1024]{2,1,0:T(8,128)(2,1)}, f32[3072]...) custom-call(s32[16]{0:T(128)} %kind_ref.3, f32[8,1040,384]{2,1,0:T(8,128)} %bitcast.3, ...), custom_call_target="tpu_custom_call" | custom-call | tf_op jit(solution)/shard_map/unpack/pallas_call | solution.py:697
where the time goes:
time: 219 us; the launch traced here: 218 us
  Pallas kernels  217 us (99%)
    pallas_call x1, Pallas kernels, layer_call(): pl.pallas_call(layer_kernel, out_shape=(tok, tok, jax.ShapeDtypeStruct((4...  203 us
    pallas_call x1, Pallas kernels, unpack_call(): pl.pallas_call(unpack_kernel, in_specs=[sm, hb, hb, hb, hb, vm], out_spec...  14.1 us

commit v1 on v0

--- a/solution.py
+++ b/solution.py
@@ -20,7 +20,7 @@
 DR = 1040
 HR = 520
 N = 16
-R3, R4, R8 = range(3), range(4), range(8)
+R2, R3, R4, R8 = range(2), range(3), range(4), range(8)
 MESH = pl.DeviceIdType.MESH
 H_ROWS = (0, 96, 176, 256)
 W_ROWS = (0, 176, 352, 520)
@@ -153,6 +153,15 @@
             to = (me + r) % N
             rcopy(self.src(to), self.dst(me), self.send, self.recv, to).start()
 
+    def start_half(self, upper):
+        me = self.place.me
+        for r in range(1, N):
+            to = (me + r) % N
+
+            @pl.when(to // 8 == upper)
+            def _():
+                rcopy(self.src(to), self.dst(me), self.send, self.recv, to).start()
+
     def wait(self):
         rcopy(self.rest, self.rest, self.send, self.recv, self.place.me).wait_recv()
 
@@ -179,13 +188,13 @@
     return xf, cen * rstd, rstd
 
 
-def layer_kernel(kind_ref, x_ref, dy_ref, gamma_ref, beta_ref, bout_ref, bqkv_ref, wqkv_hbm, wout_hbm,
-                 y_ref, dx_ref, small_ref, dwg_ref, dwo_ref,
+def layer_kernel(kind_ref, x_hbm, dy_hbm, gamma_ref, beta_ref, bout_ref, bqkv_ref, wqkv_hbm, wout_hbm,
+                 y_hbm, dx_hbm, small_ref, dwg_ref, dwo_ref, x_ref, dy_ref, y_ref, dx_ref,
                  hg_ref, out_ref, wout_ref, wp_ref, do_ref, dog_ref, w_ref, bias_ref, qkv_ref, dqkv_ref, qt_ref, dot_ref,
                  dkt_ref, dvt_ref, s_f, p_f, ds_f, s_g, p_g, ds_g, so_ref, sd_ref, ro_ref, rd_ref, o_nat, dqkv_nat,
                  dwp_ref, dws_ref, part_ref, px_ref, acc_ref, rs0_ref, rs1_ref, rs2_ref, sm_ref, sm_out,
                  loc, sib_send, sib_recv, h_send, h_recv, do_send, do_recv, o_send, o_recv, d_send, d_recv,
-                 s_send, s_recv, w_send, w_recv, g_send, g_recv, ws_send, ws_recv, gs_send, gs_recv, r_send, r_recv):
+                 s_send, s_recv, w_send, w_recv, g_send, g_recv, ws_send, ws_recv, gs_send, gs_recv, r_send, r_recv, io_sem):
     pc = Place()
     barrier_signal(pc)
 
@@ -193,6 +202,11 @@
         return pltpu.make_async_copy(wqkv_hbm.at[r * T:(r + 1) * T], dqkv_nat, loc.at[r])
 
     wo_load = pltpu.make_async_copy(wout_hbm, wout_ref, loc.at[2])
+    x_load, dy_load, y_put, dx_put = [
+        pltpu.make_async_copy(a, b, io_sem.at[i]) for i, (a, b) in enumerate(
+            ((x_hbm, x_ref), (dy_hbm, dy_ref), (y_ref, y_hbm), (dx_ref, dx_hbm)))]
+    x_load.start()
+    dy_load.start()
     w_load(0).start()
     wo_load.start()
     gamma = gamma_ref[...].reshape(1, D).astype(F32)
@@ -209,12 +223,13 @@
     def sib_copy(j):
         return rcopy(out_ref.at[j], hg_ref.at[pc.chip, j, rows_of(pc.core)], sib_send.at[j], sib_recv.at[j], pc.sib)
 
-    for j in range(2):
+    x_load.wait()
+    for j in R2:
         out_ref[j] = norm(x_ref[2 * (1 - pc.core) + j])
-    for j in range(2):
+    for j in R2:
         hg_ref[pc.chip, j, rows_of(pc.core)] = norm(x_ref[2 * pc.core + j])
     barrier_wait()
-    for j in range(2):
+    for j in R2:
         sib_copy(j).start()
 
     h_rows, w_rows, o_rows = span(H_ROWS), span(W_ROWS), span(O_ROWS)
@@ -256,18 +271,19 @@
         f = f + jnp.where(pc.chip == c, perm[c], 0)
         g = g + jnp.where(pc.chip == c, perm[8 + c], 0)
     wo_load.wait()
+    dy_load.wait()
     dy_all = dy_ref[...].reshape(T, D)
     for c in R4:
-        for u in range(2):
+        for u in R2:
             wp_ref[u * L:u * L + 64] = wout_ref[perm[2 * c + u]]
             wp_ref[u * L + 64:u * L + L] = wout_ref[perm[8 + 2 * c + u]]
         d = dot_nt(dy_all, wp_ref[...]).astype(BF)
-        for u in range(2):
+        for u in R2:
             do_ref[2 * c + u] = d[:, u * L:(u + 1) * L].reshape(4, L, L)
     for e in trees[0].hops(0):
         trees[0].arrive(e)
     do_swap(0).start()
-    for j in range(2):
+    for j in R2:
         dog_ref[j, pc.me] = do_out[pc.me, j]
 
     def w_cols(t, k, head):
@@ -277,7 +293,7 @@
             out = cur if out is None else jnp.where(head // 2 == m, cur, out)
         return out
 
-    for r in range(2):
+    for r in R2:
         w_load(r).wait()
         for t in R3:
             for k in R4:
@@ -387,7 +403,7 @@
             og, dqg = head_block(j, i, 1)
             o = jnp.where(lane < 64, of, og).astype(BF)
             dq = jnp.where(lane < 64, dqf, dqg).astype(BF)
-            for u in range(2):
+            for u in R2:
                 so_ref[j, 2 * i + u] = o[u * L:(u + 1) * L]
                 sd_ref[j, 2 * i + u, 0] = dq[u * L:(u + 1) * L]
             dqkv_ref[i * QB:(i + 1) * QB, 0:L] = dq
@@ -398,6 +414,10 @@
                         trees[1].arrive(e)
                     do_swap(1).start()
 
+                @pl.when(j == 1)
+                def _():
+                    o_swap(1).start_half(0)
+
         for t, src in ((1, dkt_ref), (2, dvt_ref)):
             for n in range(N):
                 d = src[:, n * L:(n + 1) * L].T.astype(BF)
@@ -413,7 +433,7 @@
 
         @pl.when(j == 1)
         def _():
-            o_swap(1).start()
+            o_swap(1).start_half(1)
 
         def dw_step(r, c):
             cols = pl.ds(pl.multiple_of(r * QB, QB), QB)
@@ -435,7 +455,7 @@
         return cp
 
     half = to_sib(2, half_of(1 - pc.core), dws_ref, sib_send, sib_recv)
-    for j in range(2):
+    for j in R2:
         trees[j].finish()
         do_swap(j).finish()
     w_flat = hg_ref.reshape(2 * S, D)
@@ -458,7 +478,7 @@
     for p in R3:
         to_sib(0, dws_ref.at[w_rows(p)], w_slot(pc.chip, p), ws_send, ws_recv)
 
-    for j in range(2):
+    for j in R2:
         o_swap(j).wait()
     for b in R4:
         for m in R8:
@@ -468,10 +488,10 @@
         cols = pl.ds(pl.multiple_of(core * T + c * QB, QB), QB)
         return dot_tn(o_nat[:, cols], dy_all)
 
-    for c in range(2):
+    for c in R2:
         part_ref[c * QB:(c + 1) * QB] = wout_part(1 - pc.core, c)
     xp = to_sib(3, part_ref, px_ref, sib_send, sib_recv)
-    for c in range(2):
+    for c in R2:
         acc_ref[4 * c:4 * c + 4] = wout_part(pc.core, c).reshape(4, 64, D)
     xp.wait_recv()
     acc_ref[...] += px_ref[...].reshape(8, 64, D)
@@ -503,6 +523,7 @@
         rows = slice(b * L, (b + 1) * L)
         y_ref[b] = (x_ref[b].astype(F32) + dot_nn(o_nat[rows], wout_ref.reshape(D, D)[...]) + bout).astype(BF)
         dbo += jnp.sum(dy_ref[b].astype(F32), axis=0, keepdims=True)
+    y_put.start()
     reduce_step(0, True)
     reduce_step(1, False)
     d_swap(1).start(1, 9)
@@ -518,7 +539,7 @@
         to_sib(0, acc_ref.at[pc.chip, o_rows(p)], g_slot(pc.chip, p), gs_send, gs_recv)
 
     pass_on(wtree, w_slot, 0, ws_send, ws_recv)
-    for j in range(2):
+    for j in R2:
         d_swap(j).wait()
 
     def spread(b, c):
@@ -549,6 +570,7 @@
     dgb = lax.fori_loop(0, 2, back, (jnp.zeros((1, D), F32), jnp.zeros((1, D), F32)))
     pass_on(gtree, g_slot, 0, gs_send, gs_recv)
     dg, db = lax.fori_loop(2, 4, back, dgb)
+    dx_put.start()
     row = lax.broadcasted_iota(jnp.int32, (4, D), 0)
     sm_out[...] = jnp.where(row == 0, dg, jnp.where(row == 1, db, jnp.where(row == 2, dbo, 0.0)))
     sm_ref[pc.me] = sm_out[...]
@@ -569,7 +591,7 @@
         rcopy(got, got, send.at[0], recv.at[0], pc.sib).wait_recv()
         rcopy(at, at, send.at[0], recv.at[0], pc.sib).wait_send()
         tree.finish()
-    for j in range(2):
+    for j in R2:
         sib_copy(j).wait_send()
         o_swap(j).finish()
         d_swap(j).finish()
@@ -577,8 +599,8 @@
     half.wait_send()
     xp.wait_send()
     rcopy(acc_ref.at[0:7], acc_ref.at[0:7], r_send.at[0], r_recv.at[0], pc.sib).wait_send()
-    keep_w.wait()
-    keep_g.wait()
+    for cp in (keep_w, keep_g, y_put, dx_put):
+        cp.wait()
 
 
 def layer_call(kind, x, dy, gamma, beta, bout, bqkv, wqkv, wout):
@@ -600,9 +622,9 @@
         layer_kernel,
         out_shape=(tok, tok, jax.ShapeDtypeStruct((4, D), F32), jax.ShapeDtypeStruct((8, 2, HR, W3), F32),
                    jax.ShapeDtypeStruct((2, 8, 64, D), F32)),
-        in_specs=[sm] + [vm] * 6 + [hb, hb],
-        out_specs=(vm, vm, vm, hb, hb),
-        scratch_shapes=[
+        in_specs=[sm, hb, hb] + [vm] * 4 + [hb, hb],
+        out_specs=(hb, hb, vm, hb, hb),
+        scratch_shapes=[bf(4, L, D)] * 4 + [
             bf(8, 2, QB, D), bf(2, L, D), bf(N, 64, D), bf(QB, D), bf(8, 4, L, L), bf(2, N, L, L), bf(D, W3), ff(8, W3),
             bf(S, W3), bf(S, W3), bf(L, S), bf(L, S), ff(L, S), ff(L, S),
             ff(QB, S), bf(QB, S), bf(QB, S), ff(QB, band), bf(QB, band), bf(QB, band),
@@ -610,7 +632,7 @@
             ff(DR, W3), ff(HR, W3), ff(T, D), ff(T, D), ff(8, 64, D),
             ff(4, 64, D), ff(2, 64, D), ff(1, 64, D), ff(N, 4, D), ff(4, D), sem((6,))]
         + pair(4) + [sem((2,)), sem((2, 21))] + pair(2) + pair(2) + pair(2) + pair(1)
-        + [sem((1,)), sem((21,))] + [sem((1,)), sem((21,))] + pair(1) + pair(1) + [sem((1,)), sem((9,))],
+        + [sem((1,)), sem((21,))] + [sem((1,)), sem((21,))] + pair(1) + pair(1) + [sem((1,)), sem((9,)), sem((4,))],
         compiler_params=pltpu.CompilerParams(vmem_limit_bytes=VMEM_CAP, collective_id=0, has_side_effects=True),
         name="layer",
     )(kind, x, dy, gamma, beta, bout, bqkv, wqkv, wout)

time: 219 us -> 219 us (level)
  no operation moved by 1% of the time
where the time goes in v1:
time: 219 us; the launch traced here: 217 us
  Pallas kernels  217 us (99%)
    pallas_call x1, Pallas kernels, layer_call(): pl.pallas_call(layer_kernel, out_shape=(tok, tok, jax.ShapeDtypeStruct((4...  202 us
    pallas_call x1, Pallas kernels, unpack_call(): pl.pallas_call(unpack_kernel, in_specs=[sm, hb, hb, hb, hb, vm], out_spec...  14.1 us

profile of v1, /device:TPU:0, one launch (start us, length us, event | category | flops | bytes accessed | tf_op | source)
XLA Modules:
  0.0 217.5 jit_solution(5890986074189157132)
XLA Ops:
  0.6 202.5 %layer.1 = (bf16[4,128,1024]{2,1,0:T(8,128)(2,1)}, bf16[4,128,1024]{2,1,0:T(8,128)(2,1)}, f32[4,1024]{1,0:T(4,128)}, f32[8,2,520,384]{3,2,1,0:T(8,128)}, f32[2,8,64,1024]{3,2,1,0:T(8,128)}) custom-call(s32[16]{0:T(128)} %kind_ref.3, bf16[4,128,1024]{2,1,0:T(8,128)(2,1)} %x_hbm.1, bf16[4,128,1024]{2,1,0:T(8,128)(2,1)} %dy_hbm.1, bf16[1024]{0:T(1024)(128)(2,1)} %gamma_ref.1, ...), custom_call_target="tpu_custom_call" | custom-call | tf_op jit(solution)/shard_map/layer/pallas_call | solution.py:621
  203.1 14.1 %unpack.1 = (f32[1024,3072]{1,0:T(8,128)}, f32[1024,1024]{1,0:T(8,128)}, bf16[4,128,1024]{2,1,0:T(8,128)(2,1)}, bf16[4,128,1024]{2,1,0:T(8,128)(2,1)}, f32[3072]...) custom-call(s32[16]{0:T(128)} %kind_ref.3, f32[8,1040,384]{2,1,0:T(8,128)} %bitcast.3, ...), custom_call_target="tpu_custom_call" | custom-call | tf_op jit(solution)/shard_map/unpack/pallas_call | solution.py:719

commit v2 on v1

--- a/solution.py
+++ b/solution.py
@@ -426,21 +426,22 @@
         ro_ref[j, pc.me] = so_ref[j, pc.me]
         rd_ref[j, pc.me] = sd_ref[j, pc.me]
 
+        @pl.when(j == 1)
+        def _():
+            o_swap(1).start_half(1)
+
+        def dw_step(r, c):
+            cols = pl.ds(pl.multiple_of(r * QB, QB), QB)
+            dwp_ref[cols, :] += dot_tn(hg_ref[:, j, :, cols].reshape(S, QB), dqkv_ref[...])
+            return c
+
+        lax.fori_loop(0, 4, dw_step, 0)
+
         @pl.when(j == 0)
         def _():
             for e in trees[1].hops(1):
                 trees[1].arrive(e)
 
-        @pl.when(j == 1)
-        def _():
-            o_swap(1).start_half(1)
-
-        def dw_step(r, c):
-            cols = pl.ds(pl.multiple_of(r * QB, QB), QB)
-            dwp_ref[cols, :] += dot_tn(hg_ref[:, j, :, cols].reshape(S, QB), dqkv_ref[...])
-            return c
-
-        lax.fori_loop(0, 4, dw_step, 0)
         dwp_ref[D:D + 1, :] += jnp.sum(dqkv_ref[...].astype(F32), axis=0, keepdims=True)
         return carry
 

time: 219 us -> 220 us (level)
  no operation moved by 1% of the time
where the time goes in v2:
time: 220 us; the launch traced here: 219 us
  Pallas kernels  218 us (99%)
    pallas_call x1, Pallas kernels, layer_call(): pl.pallas_call(layer_kernel, out_shape=(tok, tok, jax.ShapeDtypeStruct((4...  204 us
    pallas_call x1, Pallas kernels, unpack_call(): pl.pallas_call(unpack_kernel, in_specs=[sm, hb, hb, hb, hb, vm], out_spec...  14.1 us

profile of v2, /device:TPU:0, one launch (start us, length us, event | category | flops | bytes accessed | tf_op | source)
XLA Modules:
  0.0 218.5 jit_solution(15567359791912101477)
XLA Ops:
  0.6 203.6 %layer.1 = (bf16[4,128,1024]{2,1,0:T(8,128)(2,1)}, bf16[4,128,1024]{2,1,0:T(8,128)(2,1)}, f32[4,1024]{1,0:T(4,128)}, f32[8,2,520,384]{3,2,1,0:T(8,128)}, f32[2,8,64,1024]{3,2,1,0:T(8,128)}) custom-call(s32[16]{0:T(128)} %kind_ref.3, bf16[4,128,1024]{2,1,0:T(8,128)(2,1)} %x_hbm.1, bf16[4,128,1024]{2,1,0:T(8,128)(2,1)} %dy_hbm.1, bf16[1024]{0:T(1024)(128)(2,1)} %gamma_ref.1, ...), custom_call_target="tpu_custom_call" | custom-call | tf_op jit(solution)/shard_map/layer/pallas_call | solution.py:622
  204.2 14.1 %unpack.1 = (f32[1024,3072]{1,0:T(8,128)}, f32[1024,1024]{1,0:T(8,128)}, bf16[4,128,1024]{2,1,0:T(8,128)(2,1)}, bf16[4,128,1024]{2,1,0:T(8,128)(2,1)}, f32[3072]...) custom-call(s32[16]{0:T(128)} %kind_ref.3, f32[8,1040,384]{2,1,0:T(8,128)} %bitcast.3, ...), custom_call_target="tpu_custom_call" | custom-call | tf_op jit(solution)/shard_map/unpack/pallas_call | solution.py:720
